TPU v7x, 32 devices: a whole 2x2x4 slice. The times are simulated.
32 devices in a mesh: groups: 1, ep: 32 (over z, y, x, core).
Axes of the slice: x: 2, y: 2, z: 4, core: 2. Of those that a mesh axis runs over, the one named last changes fastest.
Arguments:
- tokens: bfloat16 [2048, 2880], P(('groups', 'ep')), may hold values from -6 to 6
- routes: int32 [2048, 4], P(('groups', 'ep')), may hold values from 0 to 7, all different within a row; in each aligned block of 64 rows (0 to 63, 64 to 127, ...) at most 36 rows name the same one
- norm_gain: bfloat16 [2880], replicated, may hold values from 0.25 to 1.75
- router_weight: bfloat16 [2880, 8], replicated, may hold values from -0.02734375 to 0.02734375
- gate_up_weight: bfloat16 [32, 2880, 720], P('ep'), may hold values from -0.109375 to 0.109375
- down_weight: bfloat16 [32, 360, 2880], P('ep'), may hold values from -0.15625 to 0.15625
Outputs:
- mixed: bfloat16 [2048, 2880], P(('groups', 'ep'))
Inputs may be any that keep to these rules, and one draw needn't show every extreme that they name: `routes`: in each aligned block of 64 rows (the rows of one device), no expert is named by more than 36 rows; in some blocks one expert is named by exactly 36 rows. A row names 4 different experts.
All inputs are finite; a program needn't handle non-finite values.
Results may differ from a plain program's by a relative error of at most 0.005.
Values may be sent and summed in bfloat16 or wider, within the bound.
A program may use at most 128 MiB of HBM per device.

v0:
```python
import jax
import jax.numpy as jnp
from jax import lax
from jax.sharding import PartitionSpec as P


def shards(tokens, routes, norm_gain, router_weight, gate_up_weight, down_weight):
    tok_rows = tokens.shape[0]
    model_width = tokens.shape[1]
    top_count = routes.shape[1]
    experts = router_weight.shape[1]
    devices = lax.axis_size("ep")
    shard_count = devices // experts
    ff_dev = down_weight.shape[1]
    capacity = min(
        tok_rows, shard_count * (17 * tok_rows * top_count // (16 * experts * shard_count) + 1)
    )
    stream = tokens.astype(jnp.float32)
    mean_square = jnp.mean(stream * stream, axis=-1, keepdims=True)
    normed = (stream * lax.rsqrt(mean_square + 1e-05) * norm_gain.astype(jnp.float32)).astype(
        jnp.bfloat16
    )
    logits = jnp.dot(normed, router_weight, preferred_element_type=jnp.float32)
    expert_ids = lax.broadcasted_iota(jnp.int32, (1, 1, experts), 2)
    onehot = routes[:, :, None] == expert_ids
    chosen = jnp.sum(jnp.where(onehot, logits[:, None, :], jnp.float32(0.0)), axis=-1)
    expo = jnp.exp(chosen)
    route_prob = expo / jnp.sum(expo, axis=-1, keepdims=True)
    flat_hits = onehot.astype(jnp.int32).reshape(tok_rows * top_count, experts)
    rank_before = jnp.cumsum(flat_hits, axis=0) - flat_hits
    slot_index = jnp.sum(flat_hits * rank_before, axis=1)
    position = routes.reshape(-1) * capacity + slot_index
    slot_iota = lax.broadcasted_iota(jnp.int32, (1, experts * capacity), 1)
    placement = position[:, None] == slot_iota
    selector = (
        placement.astype(jnp.bfloat16).reshape(tok_rows, top_count, experts * capacity).sum(axis=1)
    )
    combine_weight = jnp.where(placement, route_prob.reshape(-1)[:, None], jnp.float32(0.0))
    combine_weight = combine_weight.reshape(tok_rows, top_count, experts * capacity).sum(axis=1)
    buffer = jnp.einsum("te,td->ed", selector, normed, preferred_element_type=jnp.float32).astype(
        jnp.bfloat16
    )
    buffer = buffer.reshape(experts, capacity, model_width)
    outgoing = jnp.broadcast_to(buffer[:, None], (experts, shard_count, capacity, model_width))
    outgoing = outgoing.reshape(devices, capacity, model_width)
    received = lax.all_to_all(outgoing, "ep", split_axis=0, concat_axis=0, tiled=True)
    rows_in = received.reshape(devices * capacity, model_width)
    hidden = jnp.dot(rows_in, gate_up_weight[0], preferred_element_type=jnp.float32)
    gate_part = hidden[:, :ff_dev]
    up_part = hidden[:, ff_dev:]
    activated = ((up_part + 1.0) * gate_part * jax.nn.sigmoid(1.702 * gate_part)).astype(
        jnp.bfloat16
    )
    partial_value = jnp.dot(activated, down_weight[0], preferred_element_type=jnp.float32).astype(
        jnp.bfloat16
    )
    partial_value = partial_value.reshape(devices, capacity, model_width)
    returned = lax.all_to_all(partial_value, "ep", split_axis=0, concat_axis=0, tiled=True)
    expert_sum = (
        returned.astype(jnp.float32)
        .reshape(experts, shard_count, capacity, model_width)
        .sum(axis=1)
    )
    expert_sum = expert_sum.reshape(experts * capacity, model_width)
    mixture = jnp.dot(
        combine_weight,
        expert_sum,
        precision=lax.Precision.HIGHEST,
        preferred_element_type=jnp.float32,
    )
    return (stream + mixture).astype(jnp.bfloat16)


def solution(mesh):
    in_specs = (
        P(("groups", "ep"), None),
        P(("groups", "ep"), None),
        P(),
        P(),
        P("ep", None, None),
        P("ep", None, None),
    )
    out_specs = P(("groups", "ep"), None)
    return jax.shard_map(shards, mesh=mesh, in_specs=in_specs, out_specs=out_specs, check_vma=False)
```

profile of v0, /device:TPU:0, one launch (start us, length us, event | category | flops | bytes accessed | tf_op | source)
XLA Modules:
  0.0 417.0 jit_solution(18121460770090798714)
XLA Ops:
  0.0 0.0 copy-start
  0.0 0.9 copy.23
  0.9 0.1 eq.51
  1.0 0.1 eq.47
  1.1 1.2 fusion.10
  2.3 0.7 convert_element_type.39
  3.0 0.6 reduce-window.6
  3.6 0.2 slice_reduce_fusion
  3.9 0.1 fusion.19
  4.0 0.1 reduce_sum.69
  4.1 0.1 copy.25
  4.1 0.7 multiply_add_fusion
  4.8 0.1 fusion.14
  5.0 2.8 convolution_convert_fusion.1
  7.8 2.6 broadcast_in_dim.41
  10.4 2.0 broadcast_in_dim.42
  12.5 174.0 %all_to_all.10 = bf16[32,36,2880]{2,1,0:T(8,128)(2,1)} all-to-all(bf16[32,36,2880]{2,1,0:T(8,128)(2,1)S(1)} %bitcast.23), channel_id=1, replica_groups=mesh['groups'=1,'ep'=32] {'ep'}, dimensions={0} | all-to-all | bytes 13271040 | tf_op jit(solution)/shard_map/all_to_all | solution.py:46
  186.4 9.3 %reshape.92 = bf16[1152,2880]{1,0:T(8,128)(2,1)} reshape(bf16[32,36,2880]{2,1,0:T(8,128)(2,1)} %all_to_all.10) | data formatting | bytes 13271040 | tf_op jit(solution)/shard_map/reshape | solution.py:47
  195.8 9.7 %fusion = f32[1152,720]{0,1:T(8,128)S(1)} fusion(bf16[1152,2880]{1,0:T(8,128)(2,1)} %reshape.92, bf16[1,2880,720]{1,2,0:T(8,128)(2,1)} %param.10), kind=kOutput, calls=%fused_computation.2 | convolution fusion | flops 4777574400 | bytes 14100480 | tf_op jit(solution)/shard_map/dot_general | solution.py:48
  205.5 0.0 copy-done
  205.5 6.3 %convolution_convert_fusion = bf16[1152,2880]{0,1:T(8,128)(2,1)} fusion(bf16[1,360,2880]{2,1,0:T(8,128)(2,1)S(1)} %copy-done, f32[1152,720]{0,1:T(8,128)S(1)} %fusion), kind=kOutput, calls=%fused_computation.1 | convolution fusion | flops 2395422720 | bytes 12026880 | tf_op jit(solution)/shard_map/dot_general | solution.py:54
  211.8 10.1 %copy.26 = bf16[1152,2880]{1,0:T(8,128)(2,1)} copy(bf16[1152,2880]{0,1:T(8,128)(2,1)} %convolution_convert_fusion) | data formatting | bytes 13271040 | tf_op jit(solution)/shard_map/convert_element_type | solution.py:54
  221.9 8.7 %reshape.93 = bf16[32,36,2880]{2,1,0:T(8,128)(2,1)} reshape(bf16[1152,2880]{1,0:T(8,128)(2,1)} %copy.26) | data formatting | bytes 13271040 | tf_op jit(solution)/shard_map/reshape | solution.py:57
  230.6 0.0 copy-start.2
  230.6 0.0 copy-start.4
  230.6 0.0 copy-start.3
  230.6 3.8 all-to-all-start.1
  234.4 0.0 copy-done.2
  234.4 0.0 copy-done.4
  234.4 0.3 fusion.16
  234.7 0.0 copy-done.3
  234.7 0.1 select_reduce_fusion
  234.9 166.9 %all-to-all-done.1 = bf16[32,36,2880]{2,1,0:T(8,128)(2,1)} async-done(((bf16[32,36,2880]{2,1,0:T(8,128)(2,1)}), bf16[32,36,2880]{2,1,0:T(8,128)(2,1)}, u32[]{:S(2)}, u32[]{:S(2)}) %all-to-all-start.1) | async-done | bytes 6635552 | tf_op jit(solution)/shard_map/all_to_all | solution.py:58
  401.8 6.7 %convert_reduce_fusion = f32[8,36,2880]{2,1,0:T(8,128)} fusion(bf16[32,36,2880]{2,1,0:T(8,128)(2,1)} %all-to-all-done.1), kind=kLoop, calls=%fused_computation | loop fusion | flops 5806080 | bytes 9953280 | tf_op jit(solution)/shard_map/reduce_sum | solution.py:62
  408.4 0.0 copy-start.1
  408.4 3.6 reshape.96
  412.0 5.0 %fusion.2 = bf16[64,2880]{1,0:T(8,128)(2,1)} fusion(f32[64,288]{1,0:T(8,128)S(1)} %select_reduce_fusion, f32[288,2880]{1,0:T(8,128)} %reshape.96, bf16[64,2880]{1,0:T(8,128)(2,1)S(1)} %copy-done.2), kind=kOutput, calls=%fused_computation.6 | convolution fusion | flops 637562880 | bytes 4128768 | tf_op jit(solution)/shard_map/dot_general | solution.py:65
  417.0 0.0 copy-done.1
  (7 shorter events, 0.1 us)
Async XLA Ops:
  0.0 205.5 %copy-start = (bf16[1,360,2880]{2,1,0:T(8,128)(2,1)S(1)}, bf16[1,360,2880]{2,1,0:T(8,128)(2,1)}, u32[]{:S(2)}) copy-start(bf16[1,360,2880]{2,1,0:T(8,128)(2,1)} %param.11) | copy-start | bytes 6220804
  230.6 3.8 copy-start.2
  230.6 3.8 copy-start.4
  230.6 4.1 copy-start.3
  230.6 171.2 %all-to-all-start.1 = ((bf16[32,36,2880]{2,1,0:T(8,128)(2,1)}), bf16[32,36,2880]{2,1,0:T(8,128)(2,1)}, u32[]{:S(2)}, u32[]{:S(2)}) async-start(bf16[32,36,2880]{2,1,0:T(8,128)(2,1)} %reshape.93), calls=%async_computation.1 | async-start | bytes 15073280 | tf_op jit(solution)/shard_map/all_to_all | solution.py:58
  408.4 8.6 %copy-start.1 = (bf16[1,360,2880]{2,1,0:T(8,128)(2,1)S(1)}, bf16[1,360,2880]{2,1,0:T(8,128)(2,1)}, u32[]{:S(2)}) copy-start(bf16[1,360,2880]{2,1,0:T(8,128)(2,1)} %param.11) | copy-start | bytes 6220804
where the time goes:
time: 418 us; the launch traced here: 417 us
  blocking collectives  174 us (42%)
  waiting for transfers between devices  167 us (40%)
  local copies, waits for them, and re-layouts  37.9 us (9%)
  matrix products  24.1 us (6%)
  other arithmetic  10.2 us (2%)
    all_to_all x1, blocking collectives, shards(): lax.all_to_all(outgoing, 'ep', split_axis=0, concat_axis=0, tiled=True)  174 us
    all_to_all x1, waiting for transfers between devices, shards(): lax.all_to_all(partial_value, 'ep', split_axis=0, concat_axis=0, tiled=True)  167 us
    convert_element_type x1, local copies, waits for them, and re-layouts, shards(): jnp.dot(activated, down_weight[0], preferred_element_type=jnp.float32)  10.1 us
    dot_general x1, matrix products, shards(): jnp.dot(rows_in, gate_up_weight[0], preferred_element_type=jnp.float32)  9.7 us
    reshape x1, local copies, waits for them, and re-layouts, shards(): rows_in = received.reshape(devices * capacity, model_width)  9.31 us
    reshape x1, local copies, waits for them, and re-layouts, shards(): partial_value = partial_value.reshape(devices, capacity, model_width)  8.71 us
  transfers between devices with their start and end apart: 1, of which 1 were waited for; matrix products, arithmetic and copies ran while one was open for 0% of the time, Pallas kernels for 0%

commit v1 on v0

v1 whole, which is shorter than its diff:
```python
import functools

import jax
import jax.numpy as jnp
from jax import lax
from jax.sharding import PartitionSpec as P

CHUNKS = 1


def route_weights(normed, routes, router_weight):
    experts = router_weight.shape[1]
    logits = jnp.dot(normed, router_weight, preferred_element_type=jnp.float32)
    expert_ids = lax.broadcasted_iota(jnp.int32, (1, 1, experts), 2)
    hits = jnp.any(routes[:, :, None] == expert_ids, axis=1)
    expo = jnp.where(hits, jnp.exp(logits), jnp.float32(0.0))
    return expo / jnp.sum(expo, axis=-1, keepdims=True)


def shards(tokens, routes, norm_gain, router_weight, gate_up_weight, down_weight):
    tok_rows, width = tokens.shape
    experts = router_weight.shape[1]
    devices = lax.axis_size("ep")
    shard_count = devices // experts
    ff_dev = down_weight.shape[1]
    stream = tokens.astype(jnp.float32)
    mean_square = jnp.mean(stream * stream, axis=-1, keepdims=True)
    normed = (stream * lax.rsqrt(mean_square + 1e-05) * norm_gain.astype(jnp.float32)).astype(
        jnp.bfloat16
    )
    weights = route_weights(normed, routes, router_weight)
    all_weights = lax.all_gather(weights, "ep", axis=0, tiled=False)
    expert = lax.axis_index("ep") // shard_count
    mine = lax.dynamic_slice_in_dim(all_weights, expert, 1, axis=2)
    rows = tok_rows // CHUNKS
    pieces = []
    for c in range(CHUNKS):
        part = lax.all_gather(normed[c * rows : (c + 1) * rows], "ep", axis=0, tiled=True)
        hidden = jnp.dot(part, gate_up_weight[0], preferred_element_type=jnp.float32)
        gate_part = hidden[:, :ff_dev]
        up_part = hidden[:, ff_dev:]
        scale = mine[:, c * rows : (c + 1) * rows].reshape(devices * rows, 1)
        activated = (
            (up_part + 1.0) * gate_part * jax.nn.sigmoid(1.702 * gate_part) * scale
        ).astype(jnp.bfloat16)
        partial_value = jnp.dot(
            activated, down_weight[0], preferred_element_type=jnp.float32
        ).astype(jnp.bfloat16)
        pieces.append(lax.psum_scatter(partial_value, "ep", scatter_dimension=0, tiled=True))
    mixture = jnp.concatenate(pieces, axis=0) if CHUNKS > 1 else pieces[0]
    return (stream + mixture.astype(jnp.float32)).astype(jnp.bfloat16)


def solution(mesh):
    in_specs = (
        P(("groups", "ep"), None),
        P(("groups", "ep"), None),
        P(),
        P(),
        P("ep", None, None),
        P("ep", None, None),
    )
    out_specs = P(("groups", "ep"), None)
    return jax.shard_map(shards, mesh=mesh, in_specs=in_specs, out_specs=out_specs, check_vma=False)
```

time: 418 us -> 294 us (0.70)
  blocking collectives: 174 us -> 44.3 us
  local copies, waits for them, and re-layouts: 37.9 us -> 0.13 us
  waiting for transfers between devices: 167 us -> 204 us
  between operations: 0.11 us -> 13.5 us
    all_to_all x1 -> x0, blocking collectives: 174 us -> none  [shards(): lax.all_to_all(outgoing, 'ep', split_axis=0, concat_axis=0, tiled=True)]
    all_to_all x1 -> x0, waiting for transfers between devices: 167 us -> none  [shards(): lax.all_to_all(partial_value, 'ep', split_axis=0, concat_axis=0, tiled=True)]
    reduce_scatter x0 -> x1, waiting for transfers between devices: none -> 155 us  [shards(): lax.psum_scatter(partial_value, 'ep', scatter_dimension=0, tiled=True)]
    all_gather x0 -> x1, waiting for transfers between devices: none -> 49.6 us  [shards(): lax.all_gather(normed[c * rows:(c + 1) * rows], 'ep', axis=0, tiled=True)]
    all_gather x0 -> x1, blocking collectives: none -> 44.3 us  [shards(): all_weights = lax.all_gather(weights, 'ep', axis=0, tiled=False)]
    reshape x3 -> x0, local copies, waits for them, and re-layouts: 21.6 us -> none  [the longest x1 9.31 us: shards(): rows_in = received.reshape(devices * capacity, model_width)]
    convert_element_type x1 -> x0, local copies, waits for them, and re-layouts: 10.1 us -> none  [shards(): jnp.dot(activated, down_weight[0], preferred_element_type=jnp.float32)]
    reduce_sum x6 -> x0, other arithmetic: 7.05 us -> none  [the longest x1 6.65 us: shards(): expert_sum = returned.astype(jnp.float32).reshape(experts, shard_count, c...]
  transfers between devices with their start and end apart: 1 -> 2, of which waited for: 1 -> 2; matrix products, arithmetic and copies ran while one was open for 0% -> 1% of each run, Pallas kernels for 0% -> 0%
where the time goes in v1:
time: 294 us; the launch traced here: 293 us
  waiting for transfers between devices  204 us (69%)
  blocking collectives  44.3 us (15%)
  matrix products  24.5 us (8%)
  between operations  13.5 us (5%)
  other arithmetic  6.45 us (2%)
    reduce_scatter x1, waiting for transfers between devices, shards(): lax.psum_scatter(partial_value, 'ep', scatter_dimension=0, tiled=True)  155 us
    all_gather x1, waiting for transfers between devices, shards(): lax.all_gather(normed[c * rows:(c + 1) * rows], 'ep', axis=0, tiled=True)  49.6 us
    all_gather x1, blocking collectives, shards(): all_weights = lax.all_gather(weights, 'ep', axis=0, tiled=False)  44.3 us
    dot_general x1, matrix products, shards(): jnp.dot(part, gate_up_weight[0], preferred_element_type=jnp.float32)  13.5 us
    dot_general x1, matrix products, shards(): jnp.dot(activated, down_weight[0], preferred_element_type=jnp.float32)  9.78 us
  transfers between devices with their start and end apart: 2, of which 2 were waited for; matrix products, arithmetic and copies ran while one was open for 1% of the time, Pallas kernels for 0%

profile of v1, /device:TPU:0, one launch (start us, length us, event | category | flops | bytes accessed | tf_op | source)
XLA Modules:
  0.0 293.3 jit_solution(11948525875130946235)
XLA Ops:
  6.5 0.0 copy-start
  6.5 0.0 all-gather.4.cloned.1.call-start
  6.5 0.8 convert_element_type.22
  7.4 1.2 fusion.12
  8.6 1.9 fusion.14
  10.5 0.0 all-gather.4.cloned.1.call-update
  10.5 0.0 reduce-scatter.2.cloned.1.call-start
  10.6 0.7 fusion.16
  11.2 1.2 fusion.19
  12.5 44.3 %all-gather.1 = f32[32,64,8]{1,2,0:T(8,128)S(1)} all-gather(f32[1,64,8]{1,2,0:T(8,128)S(1)} %divide_bitcast_fusion), channel_id=2, replica_groups=mesh['groups'=1,'ep'=32] {'ep'}, dimensions={0}, use_global_device_ids=true | all-gather | bytes 67584 | tf_op jit(solution)/shard_map/all_gather | solution.py:32
  56.8 0.1 dynamic-slice_reduce_fusion
  56.9 0.1 mul.50
  56.9 49.6 %all-gather.4.cloned.1.call-done = bf16[2048,2880]{1,0:T(8,128)(2,1)} async-done(((bf16[64,2880]{1,0:T(8,128)(2,1)}), bf16[2048,2880]{1,0:T(8,128)(2,1)}) %all-gather.4.cloned.1.call-update) | async-done | bytes 11796496 | tf_op jit(solution)/shard_map/all_gather | solution.py:38
  106.6 13.5 %fusion = f32[2048,720]{0,1:T(8,128)S(1)} fusion(bf16[2048,2880]{1,0:T(8,128)(2,1)} %all-gather.4.cloned.1.call-done, bf16[1,2880,720]{1,2,0:T(8,128)(2,1)} %param.10), kind=kOutput, calls=%fused_computation.1 | convolution fusion | flops 8493465600 | bytes 21841920 | tf_op jit(solution)/shard_map/dot_general | solution.py:39
  120.1 0.0 copy-done
  120.1 9.8 %convolution_convert_fusion = bf16[2048,2880]{1,0:T(8,128)(2,1)} fusion(bf16[1,360,2880]{2,1,0:T(8,128)(2,1)S(1)} %copy-done, f32[2048,720]{0,1:T(8,128)S(1)} %fusion, f32[2048]{0:T(1024)S(1)} %mul.50), kind=kOutput, calls=%fused_computation | convolution fusion | flops 4259266560 | bytes 19776512 | tf_op jit(solution)/shard_map/dot_general | solution.py:46
  129.9 0.0 copy-start.1
  129.9 0.0 reduce-scatter.2.cloned.1.call-update
  129.9 154.7 %reduce-scatter.2.cloned.1.call-done = bf16[64,2880]{1,0:T(8,128)(2,1)} async-done(((bf16[2048,2880]{1,0:T(8,128)(2,1)}), bf16[64,2880]{1,0:T(8,128)(2,1)}) %reduce-scatter.2.cloned.1.call-update) | async-done | bytes 368656 | tf_op jit(solution)/shard_map/reduce_scatter | solution.py:49
  284.6 0.0 copy-done.1
  284.6 1.8 fusion.15
  (2 shorter events, 0.0 us)
Async XLA Ops:
  6.5 113.5 %copy-start = (bf16[1,360,2880]{2,1,0:T(8,128)(2,1)S(1)}, bf16[1,360,2880]{2,1,0:T(8,128)(2,1)}, u32[]{:S(2)}) copy-start(bf16[1,360,2880]{2,1,0:T(8,128)(2,1)} %param.11) | copy-start | bytes 6220804
  6.5 100.0 %all-gather.4.cloned.1.call-start = ((), (), s32[]{:S(2)}) async-start(), calls=%async_computation.1 | async-start | bytes 12435456 | tf_op jit(solution)/shard_map/all_gather | solution.py:38
  10.5 274.1 %reduce-scatter.2.cloned.1.call-start = ((), (), s32[]{:S(2)}) async-start(), calls=%async_computation.2 | async-start | bytes 12435456 | tf_op jit(solution)/shard_map/reduce_scatter | solution.py:49
  129.9 154.7 %copy-start.1 = (bf16[64,2880]{1,0:T(8,128)(2,1)S(1)}, bf16[64,2880]{1,0:T(8,128)(2,1)}, u32[]{:S(2)}) copy-start(bf16[64,2880]{1,0:T(8,128)(2,1)} %param.6) | copy-start | bytes 1105924
Sparse Core Ops, SparseCore 0:
  10.6 95.9 all-gather.3
  130.0 154.5 reduce-scatter.1

commit v2 on v0

v2 whole, which is shorter than its diff:
```python
import functools

import jax
import jax.numpy as jnp
from jax import lax
from jax.experimental import pallas as pl
from jax.experimental.pallas import tpu as pltpu
from jax.sharding import PartitionSpec as P

SHARD = 4
MESH = pl.DeviceIdType.MESH


def places(groups):
    me = lax.axis_index("ep")
    group = me // SHARD
    member = me % SHARD
    core = member % 2
    half = member // 2
    core_mate = me + 1 - 2 * core
    chip_mate = me + 2 - 4 * half
    return me, group, member, core, half, core_mate, chip_mate


def greet(groups, group, member, core_mate, chip_mate):
    barrier = pltpu.get_barrier_semaphore()
    others = [(group + r) % groups * SHARD + member for r in range(1, groups)]
    for other in [core_mate, chip_mate] + others:
        pl.semaphore_signal(barrier, inc=1, device_id={"ep": other}, device_id_type=MESH)
    pl.semaphore_wait(barrier, groups + 1)


def send(src, dst, sems, slot, device):
    return pltpu.make_async_remote_copy(
        src_ref=src,
        dst_ref=dst,
        send_sem=sems.at[0, slot],
        recv_sem=sems.at[1, slot],
        device_id={"ep": device},
        device_id_type=MESH,
    )


def dispatch_kernel(groups, buf, out, direct, across, paired, relayed, local):
    me, group, member, core, half, core_mate, chip_mate = places(groups)
    greet(groups, group, member, core_mate, chip_mate)
    own = pltpu.make_async_copy(buf.at[group], out.at[me], local)
    own.start()
    to_chip = [send(buf.at[group], out.at[me], across, 0, chip_mate)]
    to_chip[0].start()
    sent = []
    for r in range(1, groups):
        target = (group + r) % groups
        copy = send(buf.at[target], out.at[me], direct, r, target * SHARD + member)
        copy.start()
        sent.append(copy)
    to_core = [send(buf.at[group], out.at[me], paired, 0, core_mate)]
    to_core[0].start()
    for r in range(1, groups):
        source = (group + groups - r) % groups
        block = out.at[source * SHARD + member]
        sent[r - 1].wait_recv()
        for copies, sems, device in ((to_chip, across, chip_mate), (to_core, paired, core_mate)):
            copy = send(block, block, sems, r, device)
            copy.start()
            copies.append(copy)
    relays = []
    for r in range(groups):
        source = (group + groups - r) % groups
        block = out.at[source * SHARD + (member + 2) % SHARD]
        to_chip[r].wait_recv()
        copy = send(block, block, relayed, r, core_mate)
        copy.start()
        relays.append(copy)
    for r in range(groups):
        to_core[r].wait_recv()
        relays[r].wait_recv()
    own.wait()
    for copy in sent + to_chip + to_core + relays:
        copy.wait_send()


def dispatch(buffer, devices):
    groups, rows, width = buffer.shape
    sems = pltpu.SemaphoreType.DMA((2, groups))
    return pl.pallas_call(
        functools.partial(dispatch_kernel, groups),
        out_shape=jax.ShapeDtypeStruct((devices, rows, width), buffer.dtype),
        in_specs=[pl.BlockSpec(memory_space=pltpu.VMEM)],
        out_specs=pl.BlockSpec(memory_space=pl.ANY),
        scratch_shapes=[sems, sems, sems, sems, pltpu.SemaphoreType.DMA],
        compiler_params=pltpu.CompilerParams(collective_id=0, has_side_effects=True),
    )(buffer)


def collect_kernel(
    groups, part, out, got, summed, crossed, final, to_mate, to_chip, to_owner, local
):
    me, group, member, core, half, core_mate, chip_mate = places(groups)
    greet(groups, group, member, core_mate, chip_mate)
    order = [(group + r) % groups for r in range(groups)]
    pairs = []
    for step in range(2):
        side = (half + 1 + step) % 2
        for r in range(groups):
            slot = step * groups + r
            block = part.at[order[r] * SHARD + side * 2 + 1 - core]
            copy = send(block, got.at[slot], to_mate, slot, core_mate)
            copy.start()
            pairs.append(copy)

    def mate_sum(step, r):
        pairs[step * groups + r].wait_recv()
        side = (half + 1 + step) % 2
        mine = part[order[r] * SHARD + side * 2 + core].astype(jnp.float32)
        return mine + got[step * groups + r].astype(jnp.float32)

    crossing = [send(summed.at[r], crossed.at[r], to_chip, r, chip_mate) for r in range(groups)]
    for r in range(groups):
        summed[r] = mate_sum(0, r).astype(summed.dtype)
        if r > 0:
            crossing[r - 1].start()
    for r in range(groups):
        final[r] = mate_sum(1, r).astype(final.dtype)
        if r == 0:
            crossing[groups - 1].start()
    homing = [
        send(final.at[r], out.at[group], to_owner, r, order[r] * SHARD + member)
        for r in range(1, groups)
    ]
    own = pltpu.make_async_copy(final.at[0], out.at[group], local)
    for r in range(groups):
        crossing[r].wait_recv()
        total = final[r].astype(jnp.float32) + crossed[r].astype(jnp.float32)
        final[r] = total.astype(final.dtype)
        if r == 1:
            own.start()
        if r > 1:
            homing[r - 2].start()
    homing[groups - 2].start()
    for r in range(1, groups):
        homing[r - 1].wait_recv()
    own.wait()
    for copy in pairs + crossing + homing:
        copy.wait_send()


def collect(partial_value, groups):
    devices, rows, width = partial_value.shape
    dtype = partial_value.dtype
    return pl.pallas_call(
        functools.partial(collect_kernel, groups),
        out_shape=jax.ShapeDtypeStruct((groups, rows, width), dtype),
        in_specs=[pl.BlockSpec(memory_space=pltpu.VMEM)],
        out_specs=pl.BlockSpec(memory_space=pl.ANY),
        scratch_shapes=[
            pltpu.VMEM((2 * groups, rows, width), dtype),
            pltpu.VMEM((groups, rows, width), dtype),
            pltpu.VMEM((groups, rows, width), dtype),
            pltpu.VMEM((groups, rows, width), dtype),
            pltpu.SemaphoreType.DMA((2, 2 * groups)),
            pltpu.SemaphoreType.DMA((2, groups)),
            pltpu.SemaphoreType.DMA((2, groups)),
            pltpu.SemaphoreType.DMA,
        ],
        compiler_params=pltpu.CompilerParams(
            collective_id=1, has_side_effects=True, vmem_limit_bytes=60 * 1024 * 1024
        ),
    )(partial_value)


def shards(tokens, routes, norm_gain, router_weight, gate_up_weight, down_weight):
    tok_rows, width = tokens.shape
    top_count = routes.shape[1]
    experts = router_weight.shape[1]
    devices = lax.axis_size("ep")
    ff_dev = down_weight.shape[1]
    capacity = min(tok_rows, SHARD * (17 * tok_rows * top_count // (16 * experts * SHARD) + 1))
    capacity = -(-capacity // 8) * 8
    stream = tokens.astype(jnp.float32)
    mean_square = jnp.mean(stream * stream, axis=-1, keepdims=True)
    normed = (stream * lax.rsqrt(mean_square + 1e-05) * norm_gain.astype(jnp.float32)).astype(
        jnp.bfloat16
    )
    logits = jnp.dot(normed, router_weight, preferred_element_type=jnp.float32)
    expert_ids = lax.broadcasted_iota(jnp.int32, (1, 1, experts), 2)
    hits = jnp.any(routes[:, :, None] == expert_ids, axis=1)
    expo = jnp.where(hits, jnp.exp(logits), jnp.float32(0.0))
    prob = expo / jnp.sum(expo, axis=-1, keepdims=True)
    earlier = lax.broadcasted_iota(jnp.int32, (tok_rows, tok_rows), 1) < (
        lax.broadcasted_iota(jnp.int32, (tok_rows, tok_rows), 0)
    )
    rank = jnp.dot(
        earlier.astype(jnp.bfloat16),
        hits.astype(jnp.bfloat16),
        preferred_element_type=jnp.float32,
    ).astype(jnp.int32)
    slot = lax.broadcasted_iota(jnp.int32, (1, 1, capacity), 2)
    placed = (hits[:, :, None] & (rank[:, :, None] == slot)).reshape(tok_rows, experts * capacity)
    buffer = lax.dot_general(
        placed.astype(jnp.bfloat16),
        normed,
        (((0,), (0,)), ((), ())),
        preferred_element_type=jnp.float32,
    ).astype(jnp.bfloat16)
    received = dispatch(buffer.reshape(experts, capacity, width), devices)
    rows_in = received.reshape(devices * capacity, width)
    hidden = jnp.dot(rows_in, gate_up_weight[0], preferred_element_type=jnp.float32)
    gate_part = hidden[:, :ff_dev]
    up_part = hidden[:, ff_dev:]
    activated = ((up_part + 1.0) * gate_part * jax.nn.sigmoid(1.702 * gate_part)).astype(
        jnp.bfloat16
    )
    partial_value = jnp.dot(activated, down_weight[0], preferred_element_type=jnp.float32).astype(
        jnp.bfloat16
    )
    expert_sum = collect(partial_value.reshape(devices, capacity, width), experts)
    expert_sum = expert_sum.reshape(experts * capacity, width)
    spread = jnp.repeat(prob, capacity, axis=1) * placed.astype(jnp.float32)
    high = spread.astype(jnp.bfloat16)
    low = (spread - high.astype(jnp.float32)).astype(jnp.bfloat16)
    mixture = jnp.dot(high, expert_sum, preferred_element_type=jnp.float32) + jnp.dot(
        low, expert_sum, preferred_element_type=jnp.float32
    )
    return (stream + mixture).astype(jnp.bfloat16)


def solution(mesh):
    in_specs = (
        P(("groups", "ep"), None),
        P(("groups", "ep"), None),
        P(),
        P(),
        P("ep", None, None),
        P("ep", None, None),
    )
    out_specs = P(("groups", "ep"), None)
    return jax.shard_map(shards, mesh=mesh, in_specs=in_specs, out_specs=out_specs, check_vma=False)
```

time: 418 us -> 182 us (0.44)
  blocking collectives: 174 us -> 0 us
  waiting for transfers between devices: 167 us -> 0 us
  Pallas kernels: 0 us -> 140 us
  local copies, waits for them, and re-layouts: 37.9 us -> 10.5 us
  other arithmetic: 10.2 us -> 2.85 us
    all_to_all x1 -> x0, blocking collectives: 174 us -> none  [shards(): lax.all_to_all(outgoing, 'ep', split_axis=0, concat_axis=0, tiled=True)]
    all_to_all x1 -> x0, waiting for transfers between devices: 167 us -> none  [shards(): lax.all_to_all(partial_value, 'ep', split_axis=0, concat_axis=0, tiled=True)]
    pallas_call x0 -> x2, Pallas kernels: none -> 140 us  [the longest x1 76.5 us: collect(): pl.pallas_call(functools.partial(collect_kernel, groups), out_shape=jax.S...]
    reshape x3 -> x0, local copies, waits for them, and re-layouts: 21.6 us -> none  [the longest x1 9.31 us: shards(): rows_in = received.reshape(devices * capacity, model_width)]
    reduce_sum x6 -> x0, other arithmetic: 7.05 us -> none  [the longest x1 6.65 us: shards(): expert_sum = returned.astype(jnp.float32).reshape(experts, shard_count, c...]
    broadcast_in_dim x2 -> x0, local copies, waits for them, and re-layouts: 4.65 us -> none  [shards(): jnp.broadcast_to(buffer[:, None], (experts, shard_count, capacity, model_...]
  transfers between devices with their start and end apart: 1 -> 0, of which waited for: 1 -> 0; matrix products, arithmetic and copies ran while one was open for 0% -> 0% of each run, Pallas kernels for 0% -> 0%
where the time goes in v2:
time: 182 us; the launch traced here: 178 us
  Pallas kernels  140 us (77%)
  matrix products  24.6 us (14%)
  local copies, waits for them, and re-layouts  10.5 us (6%)
  other arithmetic  2.85 us (2%)
    pallas_call x1, Pallas kernels, collect(): pl.pallas_call(functools.partial(collect_kernel, groups), out_shape=jax.S...  76.5 us
    pallas_call x1, Pallas kernels, dispatch(): pl.pallas_call(functools.partial(dispatch_kernel, groups), out_shape=jax....  63.5 us
    convert_element_type x1, local copies, waits for them, and re-layouts, shards(): jnp.dot(activated, down_weight[0], preferred_element_type=jnp.float32)  10.4 us
    dot_general x1, matrix products, shards(): jnp.dot(rows_in, gate_up_weight[0], preferred_element_type=jnp.float32)  9.93 us
    dot_general x1, matrix products, shards(): jnp.dot(activated, down_weight[0], preferred_element_type=jnp.float32)  6.79 us

profile of v2, /device:TPU:0, one launch (start us, length us, event | category | flops | bytes accessed | tf_op | source)
XLA Modules:
  0.0 178.1 jit_solution(3522444836896017010)
XLA Ops:
  0.0 0.0 copy-start
  0.0 1.3 fusion.13
  1.3 0.7 fusion.30
  2.0 0.1 convolution_convert_fusion.2
  2.2 0.1 eq.47
  2.3 0.7 convert_element_type.43
  3.0 1.3 fusion.35
  4.3 0.1 fusion.18
  4.4 3.0 %convolution_convert_fusion.1 = bf16[320,2880]{1,0:T(8,128)(2,1)} fusion(pred[64,320]{0,1:T(32,128)(4,1)S(1)} %fusion.18, bf16[64,2880]{1,0:T(8,128)(2,1)} %param.6, f32[2880]{0:T(1024)S(1)} %convert_element_type.43, f32[64]{0:T(128)S(1)} %add_rsqrt_fusion), kind=kOutput, calls=%fused_computation.3 | convolution fusion | flops 119623680 | bytes 2244096 | tf_op jit(solution)/shard_map/dot_general | solution.py:200
  7.4 63.5 %shard_map.64 = bf16[32,40,2880]{2,1,0:T(8,128)(2,1)} custom-call(bf16[8,40,2880]{2,1,0:T(8,128)(2,1)} %bitcast.33), custom_call_target="tpu_custom_call" | custom-call | tf_op jit(solution)/shard_map/pallas_call | solution.py:86
  70.9 9.9 %fusion = f32[1280,720]{0,1:T(8,128)S(1)} fusion(bf16[1280,2880]{1,0:T(8,128)(2,1)} %bitcast.32, bf16[1,2880,720]{1,2,0:T(8,128)(2,1)} %param.10), kind=kOutput, calls=%fused_computation.1 | convolution fusion | flops 5308416000 | bytes 15206400 | tf_op jit(solution)/shard_map/dot_general | solution.py:208
  80.9 0.0 copy-done
  80.9 6.8 %convolution_convert_fusion = bf16[1280,2880]{0,1:T(8,128)(2,1)} fusion(bf16[1,360,2880]{2,1,0:T(8,128)(2,1)S(1)} %copy-done, f32[1280,720]{0,1:T(8,128)S(1)} %fusion), kind=kOutput, calls=%fused_computation | convolution fusion | flops 2661580800 | bytes 13132800 | tf_op jit(solution)/shard_map/dot_general | solution.py:214
  87.7 10.4 %copy.9 = bf16[1280,2880]{1,0:T(8,128)(2,1)} copy(bf16[1280,2880]{0,1:T(8,128)(2,1)} %convolution_convert_fusion) | data formatting | bytes 14745600 | tf_op jit(solution)/shard_map/convert_element_type | solution.py:214
  98.1 76.5 %shard_map.65 = bf16[8,40,2880]{2,1,0:T(8,128)(2,1)} custom-call(bf16[32,40,2880]{2,1,0:T(8,128)(2,1)} %bitcast.31), custom_call_target="tpu_custom_call" | custom-call | tf_op jit(solution)/shard_map/pallas_call | solution.py:151
  174.7 0.0 copy-start.1
  174.7 0.0 copy-start.2
  174.7 2.2 %convolution_bitcast_fusion.1 = f32[64,2880]{1,0:T(8,128)S(1)} fusion(bf16[8,40,2880]{2,1,0:T(8,128)(2,1)} %shard_map.65, f32[64,8]{0,1:T(8,128)S(1)} %broadcast_divide_fusion, s32[64,8]{0,1:T(8,128)S(1)} %convolution_convert_fusion.2, pred[64,8]{0,1:T(8,128)(4,1)S(1)} %fusion.30), kind=kOutput, calls=%fused_computation.7 | convolution fusion | flops 118026240 | bytes 2585088 | tf_op jit(solution)/shard_map/dot_general | solution.py:222
  176.9 0.0 copy-done.1
  176.9 0.0 copy-done.2
  176.9 1.3 fusion.4
  (3 shorter events, 0.0 us)
Async XLA Ops:
  0.0 80.9 %copy-start = (bf16[1,360,2880]{2,1,0:T(8,128)(2,1)S(1)}, bf16[1,360,2880]{2,1,0:T(8,128)(2,1)}, u32[]{:S(2)}) copy-start(bf16[1,360,2880]{2,1,0:T(8,128)(2,1)} %param.11) | copy-start | bytes 6220804
  174.7 2.2 %copy-start.1 = (bf16[8,40,2880]{2,1,0:T(8,128)(2,1)S(1)}, bf16[8,40,2880]{2,1,0:T(8,128)(2,1)}, u32[]{:S(2)}) copy-start(bf16[8,40,2880]{2,1,0:T(8,128)(2,1)} %shard_map.65) | copy-start | bytes 5529604
  174.7 2.2 %copy-start.2 = (bf16[64,2880]{1,0:T(8,128)(2,1)S(1)}, bf16[64,2880]{1,0:T(8,128)(2,1)}, u32[]{:S(2)}) copy-start(bf16[64,2880]{1,0:T(8,128)(2,1)} %param.6) | copy-start | bytes 1105924

commit v3 on v2

--- a/solution.py
+++ b/solution.py
@@ -41,6 +41,10 @@
     )
 
 
+def far_first(groups):
+    return sorted(range(groups), key=lambda r: -min(r, groups - r))
+
+
 def dispatch_kernel(groups, buf, out, direct, across, paired, relayed, local):
     me, group, member, core, half, core_mate, chip_mate = places(groups)
     greet(groups, group, member, core_mate, chip_mate)
@@ -48,27 +52,28 @@
     own.start()
     to_chip = [send(buf.at[group], out.at[me], across, 0, chip_mate)]
     to_chip[0].start()
+    turns = [1, groups - 1] + [r for r in far_first(groups) if 1 < r < groups - 1]
     sent = []
-    for r in range(1, groups):
+    for r in turns:
         target = (group + r) % groups
         copy = send(buf.at[target], out.at[me], direct, r, target * SHARD + member)
         copy.start()
         sent.append(copy)
     to_core = [send(buf.at[group], out.at[me], paired, 0, core_mate)]
     to_core[0].start()
-    for r in range(1, groups):
+    for at, r in enumerate(turns):
         source = (group + groups - r) % groups
         block = out.at[source * SHARD + member]
-        sent[r - 1].wait_recv()
+        sent[at].wait_recv()
         for copies, sems, device in ((to_chip, across, chip_mate), (to_core, paired, core_mate)):
             copy = send(block, block, sems, r, device)
             copy.start()
             copies.append(copy)
     relays = []
-    for r in range(groups):
+    for at, r in enumerate([0] + turns):
         source = (group + groups - r) % groups
         block = out.at[source * SHARD + (member + 2) % SHARD]
-        to_chip[r].wait_recv()
+        to_chip[at].wait_recv()
         copy = send(block, block, relayed, r, core_mate)
         copy.start()
         relays.append(copy)
@@ -94,66 +99,80 @@
 
 
 def collect_kernel(
-    groups, part, out, got, summed, crossed, final, to_mate, to_chip, to_owner, local
+    groups, act, weight, out, part, got, summed, crossed, final, to_mate, to_chip, to_owner, local
 ):
     me, group, member, core, half, core_mate, chip_mate = places(groups)
     greet(groups, group, member, core_mate, chip_mate)
-    order = [(group + r) % groups for r in range(groups)]
-    pairs = []
-    for step in range(2):
-        side = (half + 1 + step) % 2
-        for r in range(groups):
-            slot = step * groups + r
-            block = part.at[order[r] * SHARD + side * 2 + 1 - core]
-            copy = send(block, got.at[slot], to_mate, slot, core_mate)
-            copy.start()
-            pairs.append(copy)
-
-    def mate_sum(step, r):
-        pairs[step * groups + r].wait_recv()
-        side = (half + 1 + step) % 2
-        mine = part[order[r] * SHARD + side * 2 + core].astype(jnp.float32)
-        return mine + got[step * groups + r].astype(jnp.float32)
-
-    crossing = [send(summed.at[r], crossed.at[r], to_chip, r, chip_mate) for r in range(groups)]
-    for r in range(groups):
-        summed[r] = mate_sum(0, r).astype(summed.dtype)
-        if r > 0:
-            crossing[r - 1].start()
-    for r in range(groups):
-        final[r] = mate_sum(1, r).astype(final.dtype)
-        if r == 0:
-            crossing[groups - 1].start()
+    rows = out.shape[1]
+    chunk = SHARD * rows
+    away = far_first(groups)
+    owners = [(group + r) % groups for r in away]
+    pairs = [
+        [
+            send(
+                part.at[i, (half + 1 + side) % 2 * 2 + 1 - core],
+                got.at[2 * i + side],
+                to_mate,
+                2 * i + side,
+                core_mate,
+            )
+            for side in range(2)
+        ]
+        for i in range(groups)
+    ]
+    crossing = [send(summed.at[i], crossed.at[i], to_chip, i, chip_mate) for i in range(groups)]
+
+    def mate_sum(i, side):
+        pairs[i][side].wait_recv()
+        mine = part[i, (half + 1 + side) % 2 * 2 + core].astype(jnp.float32)
+        return (mine + got[2 * i + side].astype(jnp.float32)).astype(summed.dtype)
+
+    for step in range(groups + 2):
+        if step < groups:
+            base = pl.multiple_of(owners[step] * chunk, chunk)
+            value = jnp.dot(
+                act[pl.ds(base, chunk), :], weight[...], preferred_element_type=jnp.float32
+            )
+            for j in range(SHARD):
+                part[step, j] = value[j * rows : (j + 1) * rows].astype(part.dtype)
+        if 1 <= step <= groups:
+            for side in range(2):
+                pairs[step - 1][side].start()
+        if step >= 2:
+            summed[step - 2] = mate_sum(step - 2, 0)
+            final[step - 2] = mate_sum(step - 2, 1)
+            crossing[step - 2].start()
     homing = [
-        send(final.at[r], out.at[group], to_owner, r, order[r] * SHARD + member)
-        for r in range(1, groups)
+        send(final.at[i], out.at[group], to_owner, away[i], owners[i] * SHARD + member)
+        for i in range(groups - 1)
     ]
-    own = pltpu.make_async_copy(final.at[0], out.at[group], local)
-    for r in range(groups):
-        crossing[r].wait_recv()
-        total = final[r].astype(jnp.float32) + crossed[r].astype(jnp.float32)
-        final[r] = total.astype(final.dtype)
-        if r == 1:
+    own = pltpu.make_async_copy(final.at[groups - 1], out.at[group], local)
+    for i in range(groups):
+        crossing[i].wait_recv()
+        total = final[i].astype(jnp.float32) + crossed[i].astype(jnp.float32)
+        final[i] = total.astype(final.dtype)
+        if i < groups - 1:
+            homing[i].start()
+        else:
             own.start()
-        if r > 1:
-            homing[r - 2].start()
-    homing[groups - 2].start()
-    for r in range(1, groups):
-        homing[r - 1].wait_recv()
+    for copy in homing:
+        copy.wait_recv()
     own.wait()
-    for copy in pairs + crossing + homing:
+    for copy in [c for pair in pairs for c in pair] + crossing + homing:
         copy.wait_send()
 
 
-def collect(partial_value, groups):
-    devices, rows, width = partial_value.shape
-    dtype = partial_value.dtype
+def collect(activated, weight, groups, devices):
+    rows = activated.shape[0] // devices
+    width = weight.shape[1]
+    dtype = weight.dtype
     return pl.pallas_call(
         functools.partial(collect_kernel, groups),
         out_shape=jax.ShapeDtypeStruct((groups, rows, width), dtype),
-        in_specs=[pl.BlockSpec(memory_space=pltpu.VMEM)],
+        in_specs=[pl.BlockSpec(memory_space=pltpu.VMEM)] * 2,
         out_specs=pl.BlockSpec(memory_space=pl.ANY),
         scratch_shapes=[
+            pltpu.VMEM((groups, SHARD, rows, width), dtype),
             pltpu.VMEM((2 * groups, rows, width), dtype),
             pltpu.VMEM((groups, rows, width), dtype),
             pltpu.VMEM((groups, rows, width), dtype),
@@ -166,7 +185,7 @@
         compiler_params=pltpu.CompilerParams(
             collective_id=1, has_side_effects=True, vmem_limit_bytes=60 * 1024 * 1024
         ),
-    )(partial_value)
+    )(activated, weight)
 
 
 def shards(tokens, routes, norm_gain, router_weight, gate_up_weight, down_weight):
@@ -211,10 +230,7 @@
     activated = ((up_part + 1.0) * gate_part * jax.nn.sigmoid(1.702 * gate_part)).astype(
         jnp.bfloat16
     )
-    partial_value = jnp.dot(activated, down_weight[0], preferred_element_type=jnp.float32).astype(
-        jnp.bfloat16
-    )
-    expert_sum = collect(partial_value.reshape(devices, capacity, width), experts)
+    expert_sum = collect(activated, down_weight[0], experts, devices)
     expert_sum = expert_sum.reshape(experts * capacity, width)
     spread = jnp.repeat(prob, capacity, axis=1) * placed.astype(jnp.float32)
     high = spread.astype(jnp.bfloat16)

time: 182 us -> 148 us (0.81); the launches traced: 178 us -> 147 us
  Pallas kernels: 140 us -> 124 us
  local copies, waits for them, and re-layouts: 10.5 us -> 0.1 us
  matrix products: 24.6 us -> 17.8 us
    pallas_call x1, Pallas kernels: 76.5 us -> 55.6 us  [collect(): pl.pallas_call(functools.partial(collect_kernel, groups), out_shape=jax.S...]
    convert_element_type x1 -> x0, local copies, waits for them, and re-layouts: 10.4 us -> none  [shards(): jnp.dot(activated, down_weight[0], preferred_element_type=jnp.float32)]
    dot_general x1 -> x0, matrix products: 6.79 us -> none  [shards(): jnp.dot(activated, down_weight[0], preferred_element_type=jnp.float32)]
    pallas_call x1, Pallas kernels: 63.5 us -> 68.7 us  [dispatch(): pl.pallas_call(functools.partial(dispatch_kernel, groups), out_shape=jax....]
where the time goes in v3:
time: 148 us; the launch traced here: 147 us
  Pallas kernels  124 us (84%)
  matrix products  17.8 us (12%)
  other arithmetic  4.4 us (3%)
    pallas_call x1, Pallas kernels, dispatch(): pl.pallas_call(functools.partial(dispatch_kernel, groups), out_shape=jax....  68.7 us
    pallas_call x1, Pallas kernels, collect(): pl.pallas_call(functools.partial(collect_kernel, groups), out_shape=jax.S...  55.6 us
    dot_general x1, matrix products, shards(): jnp.dot(rows_in, gate_up_weight[0], preferred_element_type=jnp.float32)  9.88 us
    dot_general x1, matrix products, shards(): lax.dot_general(placed.astype(jnp.bfloat16), normed, (((0,), (0,)), ((),...  3.03 us

profile of v3, /device:TPU:0, one launch (start us, length us, event | category | flops | bytes accessed | tf_op | source)
XLA Modules:
  0.0 146.6 jit_solution(18328380361970656485)
XLA Ops:
  0.0 0.0 copy-start
  0.0 1.2 fusion.9
  1.2 0.7 fusion.26
  1.9 0.1 convolution_convert_fusion.1
  2.0 0.1 eq.47
  2.1 0.7 convert_element_type.40
  2.8 0.0 copy-done
  2.8 1.3 fusion.29
  4.1 0.1 fusion.14
  4.2 3.0 %convolution_convert_fusion = bf16[320,2880]{1,0:T(8,128)(2,1)} fusion(pred[64,320]{0,1:T(32,128)(4,1)S(1)} %fusion.14, bf16[64,2880]{1,0:T(8,128)(2,1)} %param.6, f32[2880]{0:T(1024)S(1)} %convert_element_type.40, f32[64]{0:T(128)S(1)} %add_rsqrt_fusion), kind=kOutput, calls=%fused_computation.2 | convolution fusion | flops 119623680 | bytes 2244096 | tf_op jit(solution)/shard_map/dot_general | solution.py:219
  7.3 68.7 %shard_map.64 = bf16[32,40,2880]{2,1,0:T(8,128)(2,1)} custom-call(bf16[8,40,2880]{2,1,0:T(8,128)(2,1)} %bitcast.29), custom_call_target="tpu_custom_call" | custom-call | tf_op jit(solution)/shard_map/pallas_call | solution.py:91
  76.0 9.9 %fusion = f32[1280,720]{1,0:T(8,128)S(1)} fusion(bf16[1280,2880]{1,0:T(8,128)(2,1)} %bitcast.28, bf16[1,2880,720]{1,2,0:T(8,128)(2,1)} %param.10), kind=kOutput, calls=%fused_computation | convolution fusion | flops 5308416000 | bytes 15206400 | tf_op jit(solution)/shard_map/dot_general | solution.py:227
  85.9 1.7 %fusion.7.act = bf16[1280,360]{1,0:T(8,128)(2,1)} fusion(f32[1280,720]{1,0:T(8,128)S(1)} %fusion), kind=kLoop, calls=%fused_computation.11 | loop fusion | flops 3686400 | bytes 4608000 | tf_op jit(solution)/shard_map/convert_element_type | solution.py:230
  87.6 55.6 %shard_map.65 = bf16[8,40,2880]{2,1,0:T(8,128)(2,1)} custom-call(bf16[1280,360]{1,0:T(8,128)(2,1)} %fusion.7.act, bf16[360,2880]{1,0:T(8,128)(2,1)} %bitcast.30), custom_call_target="tpu_custom_call" | custom-call | tf_op jit(solution)/shard_map/pallas_call | solution.py:169
  143.1 0.0 copy-start.1
  143.1 0.0 copy-start.2
  143.1 2.2 %convolution_bitcast_fusion.1 = f32[64,2880]{1,0:T(8,128)S(1)} fusion(bf16[8,40,2880]{2,1,0:T(8,128)(2,1)} %shard_map.65, f32[64,8]{0,1:T(8,128)S(1)} %broadcast_divide_fusion, s32[64,8]{0,1:T(8,128)S(1)} %convolution_convert_fusion.1, pred[64,8]{0,1:T(8,128)(4,1)S(1)} %fusion.26), kind=kOutput, calls=%fused_computation.6 | convolution fusion | flops 118026240 | bytes 2585088 | tf_op jit(solution)/shard_map/dot_general | solution.py:238
  145.3 0.0 copy-done.1
  145.3 0.0 copy-done.2
  145.4 1.3 fusion.4
  (3 shorter events, 0.0 us)
Async XLA Ops:
  0.0 2.8 %copy-start = (bf16[2880,8]{0,1:T(8,128)(2,1)S(1)}, bf16[2880,8]{0,1:T(8,128)(2,1)}, u32[]{:S(2)}) copy-start(bf16[2880,8]{0,1:T(8,128)(2,1)} %param.9) | copy-start | bytes 138244
  143.1 2.2 %copy-start.1 = (bf16[8,40,2880]{2,1,0:T(8,128)(2,1)S(1)}, bf16[8,40,2880]{2,1,0:T(8,128)(2,1)}, u32[]{:S(2)}) copy-start(bf16[8,40,2880]{2,1,0:T(8,128)(2,1)} %shard_map.65) | copy-start | bytes 5529604
  143.1 2.2 %copy-start.2 = (bf16[64,2880]{1,0:T(8,128)(2,1)S(1)}, bf16[64,2880]{1,0:T(8,128)(2,1)}, u32[]{:S(2)}) copy-start(bf16[64,2880]{1,0:T(8,128)(2,1)} %param.6) | copy-start | bytes 1105924

commit v4 on v3

--- a/solution.py
+++ b/solution.py
@@ -52,7 +52,7 @@
     own.start()
     to_chip = [send(buf.at[group], out.at[me], across, 0, chip_mate)]
     to_chip[0].start()
-    turns = [1, groups - 1] + [r for r in far_first(groups) if 1 < r < groups - 1]
+    turns = list(range(1, groups))
     sent = []
     for r in turns:
         target = (group + r) % groups

time: 148 us -> 153 us (1.034)
  Pallas kernels: 124 us -> 130 us
    pallas_call x1, Pallas kernels: 55.6 us -> 66.5 us  [collect(): pl.pallas_call(functools.partial(collect_kernel, groups), out_shape=jax.S...]
    pallas_call x1, Pallas kernels: 68.7 us -> 63.5 us  [dispatch(): pl.pallas_call(functools.partial(dispatch_kernel, groups), out_shape=jax....]
where the time goes in v4:
time: 153 us; the launch traced here: 152 us
  Pallas kernels  130 us (85%)
  matrix products  17.8 us (12%)
  other arithmetic  4.4 us (3%)
    pallas_call x1, Pallas kernels, collect(): pl.pallas_call(functools.partial(collect_kernel, groups), out_shape=jax.S...  66.5 us
    pallas_call x1, Pallas kernels, dispatch(): pl.pallas_call(functools.partial(dispatch_kernel, groups), out_shape=jax....  63.5 us
    dot_general x1, matrix products, shards(): jnp.dot(rows_in, gate_up_weight[0], preferred_element_type=jnp.float32)  9.88 us

profile of v4, /device:TPU:0, one launch (start us, length us, event | category | flops | bytes accessed | tf_op | source)
XLA Modules:
  0.0 152.4 jit_solution(5570102395044654670)
XLA Ops:
  0.0 0.0 copy-start
  0.0 1.2 fusion.9
  1.2 0.7 fusion.26
  1.9 0.1 convolution_convert_fusion.1
  2.0 0.1 eq.47
  2.1 0.7 convert_element_type.40
  2.8 0.0 copy-done
  2.8 1.3 fusion.29
  4.1 0.1 fusion.14
  4.2 3.0 %convolution_convert_fusion = bf16[320,2880]{1,0:T(8,128)(2,1)} fusion(pred[64,320]{0,1:T(32,128)(4,1)S(1)} %fusion.14, bf16[64,2880]{1,0:T(8,128)(2,1)} %param.6, f32[2880]{0:T(1024)S(1)} %convert_element_type.40, f32[64]{0:T(128)S(1)} %add_rsqrt_fusion), kind=kOutput, calls=%fused_computation.2 | convolution fusion | flops 119623680 | bytes 2244096 | tf_op jit(solution)/shard_map/dot_general | solution.py:219
  7.3 63.5 %shard_map.64 = bf16[32,40,2880]{2,1,0:T(8,128)(2,1)} custom-call(bf16[8,40,2880]{2,1,0:T(8,128)(2,1)} %bitcast.29), custom_call_target="tpu_custom_call" | custom-call | tf_op jit(solution)/shard_map/pallas_call | solution.py:91
  70.8 9.9 %fusion = f32[1280,720]{1,0:T(8,128)S(1)} fusion(bf16[1280,2880]{1,0:T(8,128)(2,1)} %bitcast.28, bf16[1,2880,720]{1,2,0:T(8,128)(2,1)} %param.10), kind=kOutput, calls=%fused_computation | convolution fusion | flops 5308416000 | bytes 15206400 | tf_op jit(solution)/shard_map/dot_general | solution.py:227
  80.7 1.7 %fusion.7.act = bf16[1280,360]{1,0:T(8,128)(2,1)} fusion(f32[1280,720]{1,0:T(8,128)S(1)} %fusion), kind=kLoop, calls=%fused_computation.11 | loop fusion | flops 3686400 | bytes 4608000 | tf_op jit(solution)/shard_map/convert_element_type | solution.py:230
  82.4 66.5 %shard_map.65 = bf16[8,40,2880]{2,1,0:T(8,128)(2,1)} custom-call(bf16[1280,360]{1,0:T(8,128)(2,1)} %fusion.7.act, bf16[360,2880]{1,0:T(8,128)(2,1)} %bitcast.30), custom_call_target="tpu_custom_call" | custom-call | tf_op jit(solution)/shard_map/pallas_call | solution.py:169
  148.9 0.0 copy-start.1
  148.9 0.0 copy-start.2
  148.9 2.2 %convolution_bitcast_fusion.1 = f32[64,2880]{1,0:T(8,128)S(1)} fusion(bf16[8,40,2880]{2,1,0:T(8,128)(2,1)} %shard_map.65, f32[64,8]{0,1:T(8,128)S(1)} %broadcast_divide_fusion, s32[64,8]{0,1:T(8,128)S(1)} %convolution_convert_fusion.1, pred[64,8]{0,1:T(8,128)(4,1)S(1)} %fusion.26), kind=kOutput, calls=%fused_computation.6 | convolution fusion | flops 118026240 | bytes 2585088 | tf_op jit(solution)/shard_map/dot_general | solution.py:238
  151.1 0.0 copy-done.1
  151.1 0.0 copy-done.2
  151.1 1.3 fusion.4
  (3 shorter events, 0.0 us)
Async XLA Ops:
  0.0 2.8 %copy-start = (bf16[2880,8]{0,1:T(8,128)(2,1)S(1)}, bf16[2880,8]{0,1:T(8,128)(2,1)}, u32[]{:S(2)}) copy-start(bf16[2880,8]{0,1:T(8,128)(2,1)} %param.9) | copy-start | bytes 138244
  148.9 2.2 %copy-start.1 = (bf16[8,40,2880]{2,1,0:T(8,128)(2,1)S(1)}, bf16[8,40,2880]{2,1,0:T(8,128)(2,1)}, u32[]{:S(2)}) copy-start(bf16[8,40,2880]{2,1,0:T(8,128)(2,1)} %shard_map.65) | copy-start | bytes 5529604
  148.9 2.2 %copy-start.2 = (bf16[64,2880]{1,0:T(8,128)(2,1)S(1)}, bf16[64,2880]{1,0:T(8,128)(2,1)}, u32[]{:S(2)}) copy-start(bf16[64,2880]{1,0:T(8,128)(2,1)} %param.6) | copy-start | bytes 1105924
